TPU v7x, 64 devices: a 2x2x8 block of a 4x4x8 slice. The times are simulated.
64 devices in a mesh: dp: 4 (over x, y), tp: 16 (over z, core).
Axes of the slice: x: 2, y: 2, z: 8, core: 2. Of those that a mesh axis runs over, the one named last changes fastest.
The devices are a block of a 4x4x8 slice.
Arguments:
- x: bfloat16 [256, 3072], P('dp'), parts along dimension 0
- k_cache: bfloat16 [256, 1024, 16, 256], P('dp', None, 'tp'), parts along dimension 0
- v_cache: bfloat16 [256, 1024, 16, 256], P('dp', None, 'tp'), parts along dimension 0
- gain_a: bfloat16 [3072], replicated
- wq: bfloat16 [3072, 4096], P(None, 'tp')
- wo: bfloat16 [4096, 3072], P('tp')
- gain_m: bfloat16 [3072], replicated
- w_gate: bfloat16 [3072, 24576], P(None, 'tp')
- w_up: bfloat16 [3072, 24576], P(None, 'tp')
- w_down: bfloat16 [24576, 3072], P('tp')
Outputs:
- output: bfloat16 [256, 3072], P('dp'), parts along dimension 0
There are 4 independent parts. A program takes and returns all parts, laid end to end along the dimension named above; an argument that names none is the same for every part.
All inputs are finite; a program needn't handle non-finite values.
Results may differ from a plain program's by a relative error of at most 0.017.
Values are sent between devices in bfloat16 or wider.
A program may use at most 768 MiB of HBM per device.

v0:
```python
import jax
import jax.numpy as jnp
from jax import lax
from jax.sharding import PartitionSpec as P

HEAD = 256
THETA = 10000


def normed(x, gain):
    wide = x.astype(jnp.float32)
    scale = lax.rsqrt(jnp.mean(wide * wide, -1, keepdims=True) + 1e-6)
    return (wide * scale * gain.astype(jnp.float32)).astype(jnp.bfloat16)


def turned(t, place, theta):
    half = t.shape[-1] // 2
    angle = place.astype(jnp.float32)[:, None] * theta ** (-jnp.arange(half, dtype=jnp.float32) / half)
    cos, sin = jnp.cos(angle)[:, None], jnp.sin(angle)[:, None]
    a, b = t[..., :half].astype(jnp.float32), t[..., half:].astype(jnp.float32)
    return jnp.concatenate([a * cos - b * sin, b * cos + a * sin], -1).astype(jnp.bfloat16)


def matmul(a, w):
    return jnp.dot(a, w, preferred_element_type=jnp.float32).astype(jnp.bfloat16)


def einsum(form, a, b):
    return jnp.einsum(form, a.astype(jnp.float32), b.astype(jnp.float32))


def seen_by(a, wq, k_cache, v_cache, head, theta):
    batch, cache, kv_heads = k_cache.shape[:3]
    place = jnp.full((batch,), cache - 1)
    q = turned(matmul(a, wq).reshape(batch, -1, head), place, theta).reshape(batch, kv_heads, -1, head)
    scores = einsum("bgsd,bugd->bgsu", q, k_cache) * head**-0.5
    weights = jax.nn.softmax(scores, -1).astype(jnp.bfloat16)
    return einsum("bgsu,bugd->bgsd", weights, v_cache).astype(jnp.bfloat16).reshape(batch, -1)


def hidden_of(b, w_gate, w_up):
    gate = jnp.dot(b, w_gate, preferred_element_type=jnp.float32)
    up = jnp.dot(b, w_up, preferred_element_type=jnp.float32)
    return (jax.nn.silu(gate) * up).astype(jnp.bfloat16)


def solution(mesh):
    def added(t, term):
        return (t.astype(jnp.float32) + lax.psum(term.astype(jnp.bfloat16), "tp").astype(jnp.float32)).astype(jnp.bfloat16)

    def step(x, k_cache, v_cache, gain_a, wq, wo, gain_m, w_gate, w_up, w_down):
        seen = seen_by(normed(x, gain_a), wq, k_cache, v_cache, HEAD, THETA)
        h = added(x, jnp.dot(seen, wo, preferred_element_type=jnp.float32))
        return added(h, jnp.dot(hidden_of(normed(h, gain_m), w_gate, w_up), w_down, preferred_element_type=jnp.float32))

    states, cache, columns, rows_of = P("dp", None), P("dp", None, "tp", None), P(None, "tp"), P("tp", None)
    return jax.shard_map(
        step,
        mesh=mesh,
        in_specs=(states, cache, cache, P(None), columns, rows_of, P(None), columns, columns, rows_of),
        out_specs=states,
        check_vma=False,
    )
```

profile of v0, /device:TPU:21, one launch (start us, length us, event | category | flops | bytes accessed | tf_op | source)
XLA Modules:
  0.0 278.9 jit_solution(5283906333346000390)
XLA Ops:
  6.5 0.0 copy-start
  6.6 0.0 all-reduce.3.cloned.1.call-start
  6.6 1.3 fusion.6
  7.9 0.7 convert_element_type.68
  8.6 2.0 fusion.5
  10.6 14.5 %fusion.2 = f32[64,1,1024]{2,1,0:T(1,128)S(1)} fusion(bf16[64,1024,1,256]{3,1,2,0:T(8,128)(2,1)} %param.11, bf16[64,256,1]{1,0,2:T(8,128)(2,1)S(1)} %maximum_bitcast_fusion), kind=kOutput, calls=%fused_computation.2 | convolution fusion | flops 33554432 | bytes 33849344 | tf_op jit(solution)/shard_map/bgsd,bugd->bgsu/dot_general | solution.py:29
  25.1 0.2 fusion.24
  25.3 0.2 fusion.23
  25.5 0.1 fusion.26
  25.6 0.0 copy-start.2
  25.6 0.0 copy-start.1
  25.6 12.9 %fusion = bf16[64,1,256]{2,1,0:T(2,128)(2,1)S(1)} fusion(bf16[64,1024,1,256]{3,1,2,0:T(8,128)(2,1)} %param.12, bf16[64,1024,1]{1,0,2:T(8,128)(2,1)S(1)} %fusion.26), kind=kOutput, calls=%fused_computation | convolution fusion | flops 33554432 | bytes 33718272 | tf_op jit(solution)/shard_map/bgsu,bugd->bgsd/dot_general | solution.py:29
  38.6 0.0 copy-done
  38.6 1.1 convolution_convert_fusion.1
  39.7 0.1 all-reduce.3.cloned.1.call-update
  39.8 0.1 all-reduce.5.cloned.1.call-start
  39.9 0.0 copy-done.2
  39.9 108.5 %all-reduce.3.cloned.1.call-done = bf16[64,3072]{1,0:T(8,128)(2,1)} async-done(((bf16[64,3072]{1,0:T(8,128)(2,1)}), bf16[64,3072]{1,0:T(8,128)(2,1)}) %all-reduce.3.cloned.1.call-update) | async-done | bytes 393232 | tf_op jit(solution)/shard_map/psum | solution.py:49
  148.4 0.0 copy-done.1
  148.4 1.2 fusion.10
  149.6 5.5 %fusion.29 = f32[64,1536]{1,0:T(8,128)S(1)} fusion(bf16[3072,1536]{1,0:T(8,128)(2,1)} %param.17, bf16[64,3072]{1,0:T(8,128)(2,1)S(1)} %get-tuple-element.6, f32[3072]{0:T(1024)S(1)} %convert_element_type.79, f32[64]{0:T(128)S(1)} %add_rsqrt_fusion), kind=kOutput, calls=%fused_computation.39 | convolution fusion | flops 604766208 | bytes 10236160 | tf_op jit(solution)/shard_map/dot_general | solution.py:42
  155.1 10.6 %convolution_convert_fusion = bf16[64,3072]{1,0:T(8,128)(2,1)} fusion(bf16[1536,3072]{1,0:T(8,128)(2,1)} %param.19, bf16[3072,1536]{1,0:T(8,128)(2,1)} %param.18, f32[64,1536]{1,0:T(8,128)S(1)} %fusion.29, bf16[64,3072]{1,0:T(8,128)(2,1)S(1)} %get-tuple-element.6, f32[3072]{0:T(1024)S(1)} %convert_element_type.79, f32[64]{0:T(128)S(1)} %add_rsqrt_fusion), kind=kOutput, calls=%fused_computation.4 | convolution fusion | flops 1209532416 | bytes 20066560 | tf_op jit(solution)/shard_map/dot_general | solution.py:54
  165.7 0.1 all-reduce.5.cloned.1.call-update
  165.8 104.5 %all-reduce.5.cloned.1.call-done = bf16[64,3072]{1,0:T(8,128)(2,1)} async-done(((bf16[64,3072]{1,0:T(8,128)(2,1)}), bf16[64,3072]{1,0:T(8,128)(2,1)}) %all-reduce.5.cloned.1.call-update) | async-done | bytes 393232 | tf_op jit(solution)/shard_map/psum | solution.py:49
  270.3 1.8 fusion.13
  (6 shorter events, 0.1 us)
Async XLA Ops:
  6.5 32.0 %copy-start = (bf16[256,3072]{1,0:T(8,128)(2,1)S(1)}, bf16[256,3072]{1,0:T(8,128)(2,1)}, u32[]{:S(2)}) copy-start(bf16[256,3072]{1,0:T(8,128)(2,1)} %param.15) | copy-start | bytes 4718596
  6.6 141.8 %all-reduce.3.cloned.1.call-start = ((), (), s32[]{:S(2)}) async-start(), calls=%async_computation | async-start | bytes 786432 | tf_op jit(solution)/shard_map/psum | solution.py:49
  25.6 14.2 %copy-start.2 = (bf16[3072]{0:T(1024)(128)(2,1)S(1)}, bf16[3072]{0:T(1024)(128)(2,1)}, u32[]{:S(2)}) copy-start(bf16[3072]{0:T(1024)(128)(2,1)} %param.16) | copy-start | bytes 18436
  25.6 122.8 %copy-start.1 = (bf16[64,3072]{1,0:T(8,128)(2,1)S(1)}, bf16[64,3072]{1,0:T(8,128)(2,1)}, u32[]{:S(2)}) copy-start(bf16[64,3072]{1,0:T(8,128)(2,1)} %param.10) | copy-start | bytes 1179652
  39.8 230.5 %all-reduce.5.cloned.1.call-start = ((), (), s32[]{:S(2)}) async-start(), calls=%async_computation.1 | async-start | bytes 786432 | tf_op jit(solution)/shard_map/psum | solution.py:49
Sparse Core Ops, SparseCore 0:
  39.9 108.4 all-reduce.2
  165.9 104.3 all-reduce.4
where the time goes:
time: 279 us
  waiting for transfers between devices  213 us (76%)
  matrix products  46.6 us (17%)
  between operations  13.5 us (5%)
  other arithmetic  5.66 us (2%)
    psum x2, waiting for transfers between devices, added(): lax.psum(term.astype(jnp.bfloat16), 'tp').astype(jnp.float32)  213 us
    dot_general x2, matrix products, einsum(): return jnp.einsum(form, a.astype(jnp.float32), b.astype(jnp.float32))  27.4 us
    dot_general x1, matrix products, step(): jnp.dot(hidden_of(normed(h, gain_m), w_gate, w_up), w_down, preferred_ele...  10.6 us
  transfers between devices with their start and end apart: 2, of which 2 were waited for; matrix products, arithmetic and copies ran while one was open for 0% of the time, Pallas kernels for 0%

commit v1 on v0

v1 whole, which is shorter than its diff:
```python
import functools

import jax
import jax.numpy as jnp
import numpy as np
from jax import lax
from jax.experimental import pallas as pl
from jax.experimental.pallas import tpu as pltpu
from jax.sharding import PartitionSpec as P

HEAD = 256
THETA = 10000
CORES = 2
GROUP = 8
CHUNK = 16
SLOTS = 3
MESH = pl.DeviceIdType.MESH
F32, BF16 = jnp.float32, jnp.bfloat16


def rotary_table(cache, half):
    angle = np.float32(cache - 1) * (np.float32(THETA) ** (-np.arange(half, dtype=np.float32) / half))
    return np.stack([np.cos(angle), np.sin(angle)]).astype(np.float32)


def layer(n, x_hbm, k_hbm, v_hbm, ga_ref, trig_ref, wq_hbm, wo_hbm, gm_ref, wg_hbm, wu_hbm, wd_hbm, out_ref,
          x16, xs, a16, wq, wo, wg, wu, wd, kbuf, vbuf, q32, s32, hb,
          send1, recv1, hg, send2, recv2, yg,
          in_sem, k_sem, v_sem, s1s, s1r, g1s, g1r, s2s, s2r, g2s, g2r):
    rows, d = x16.shape
    ff = wg.shape[1]
    groups, chunks = rows // GROUP, rows // CHUNK
    half = CHUNK // CORES
    chips = n // CORES
    cols = d // chips
    me = lax.axis_index("tp")
    z, core = me // CORES, lax.rem(me, CORES)
    tiles = d // 128

    def peer(i):
        return lax.rem(me + i, n)

    order = sorted(range(1, n), key=lambda i: -min(i, n - i))

    load_x = pltpu.make_async_copy(x_hbm, x16, in_sem.at[0])
    load_wq = pltpu.make_async_copy(wq_hbm, wq, in_sem.at[1])
    load_wo = pltpu.make_async_copy(wo_hbm, wo, in_sem.at[2])
    load_wg = pltpu.make_async_copy(wg_hbm, wg, in_sem.at[3])
    load_wu = pltpu.make_async_copy(wu_hbm, wu, in_sem.at[4])
    load_wd = pltpu.make_async_copy(wd_hbm, wd, in_sem.at[5])

    def load_k(g):
        slot = lax.rem(g, SLOTS)
        return pltpu.make_async_copy(k_hbm.at[pl.ds(g * GROUP, GROUP)], kbuf.at[slot], k_sem.at[slot])

    def load_v(g):
        slot = lax.rem(g, SLOTS)
        return pltpu.make_async_copy(v_hbm.at[pl.ds(g * GROUP, GROUP)], vbuf.at[slot], v_sem.at[slot])

    load_x.start()
    load_wq.start()
    for g in range(SLOTS):
        load_k(g).start()
        load_v(g).start()
        if g == 0:
            load_wo.start()

    barrier = pltpu.get_barrier_semaphore()
    for i in range(1, n):
        pl.semaphore_signal(barrier, inc=1, device_id={"tp": peer(i)}, device_id_type=MESH)

    load_x.wait()
    part = jnp.zeros((rows, 128), F32)
    for j in range(tiles):
        block = x16[:, pl.ds(128 * j, 128)].astype(F32)
        xs[:, pl.ds(128 * j, 128)] = block
        part += block * block
    scale = lax.rsqrt(jnp.sum(part, -1, keepdims=True) / d + 1e-6)
    gain = ga_ref[...].astype(F32)
    for j in range(tiles):
        a16[:, pl.ds(128 * j, 128)] = (xs[:, pl.ds(128 * j, 128)] * scale * gain[j:j + 1]).astype(BF16)
    load_wq.wait()
    q = jnp.dot(a16[...], wq[...], preferred_element_type=F32).astype(BF16).astype(F32)
    turn = HEAD // 2
    cos, sin = trig_ref[0:1], trig_ref[1:2]
    qa, qb = q[:, :turn], q[:, turn:]
    q32[:, :turn] = (qa * cos - qb * sin).astype(BF16).astype(F32)
    q32[:, turn:] = (qb * cos + qa * sin).astype(BF16).astype(F32)

    pl.semaphore_wait(barrier, n - 1)

    def piece(src, dst, ssem, rsem, to):
        return pltpu.make_async_remote_copy(src_ref=src, dst_ref=dst, send_sem=ssem, recv_sem=rsem,
                                            device_id={"tp": to}, device_id_type=MESH)

    def scatter1(c):
        seen = s32[pl.ds(pl.multiple_of(c * CHUNK, CHUNK), CHUNK), :].astype(BF16)
        for t in range(chips):
            term = jnp.dot(seen, wo[:, pl.ds(t * cols, cols)], preferred_element_type=F32)
            for k in range(CORES):
                send1[c, CORES * t + k] = term[half * k:half * (k + 1)].astype(BF16)
        for i in order:
            to = peer(i)
            piece(send1.at[c, to], recv1.at[c, me], s1s.at[c, to], s1r.at[c, me], to).start()

    def gather1(c):
        total = send1[c, me].astype(F32)
        for i in order:
            frm = peer(i)
            piece(send1.at[c, frm], recv1.at[c, frm], s1s.at[c, frm], s1r.at[c, frm], frm).wait_recv()
        for i in order:
            total += recv1[c, peer(i)].astype(F32)
        at = pl.ds(pl.multiple_of(c * CHUNK + core * half, half), half)
        hg[c, me] = (xs[at, pl.ds(pl.multiple_of(z * cols, 128), cols)] + total).astype(BF16)
        for i in order:
            to = peer(i)
            piece(hg.at[c, me], hg.at[c, me], g1s.at[c, to], g1r.at[c, me], to).start()

    line = lax.broadcasted_iota(jnp.int32, (GROUP, 1), 0)

    def attend(g, _):
        slot = lax.rem(g, SLOTS)
        at = pl.ds(pl.multiple_of(g * GROUP, GROUP), GROUP)
        load_k(g).wait()
        qg = q32[at, :]
        scores = None
        for i in range(GROUP):
            mine = jnp.where(line == i, qg, 0.0).astype(BF16)
            s = lax.dot_general(mine, kbuf[slot, i], (((1,), (1,)), ((), ())), preferred_element_type=F32)
            scores = s if scores is None else scores + s

        @pl.when(g + SLOTS < groups)
        def _():
            load_k(g + SLOTS).start()

        scores = scores * HEAD**-0.5
        e = jnp.exp(scores - jnp.max(scores, -1, keepdims=True))
        w = e * (1.0 / jnp.sum(e, -1, keepdims=True))
        load_v(g).wait()
        seen = None
        for i in range(GROUP):
            mine = jnp.where(line == i, w, 0.0).astype(BF16)
            s = jnp.dot(mine, vbuf[slot, i], preferred_element_type=F32)
            seen = s if seen is None else seen + s
        s32[at, :] = seen

        @pl.when(g + SLOTS < groups)
        def _():
            load_v(g + SLOTS).start()

        @pl.when(g == groups - SLOTS - 1)
        def _():
            load_wg.start()
            load_wu.start()
            load_wd.start()

        @pl.when(g == 1)
        def _():
            load_wo.wait()

        per = CHUNK // GROUP

        @pl.when(lax.rem(g, per) == per - 1)
        def _():
            scatter1(g // per)

        @pl.when((lax.rem(g, per) == 0) & (g >= 2 * per))
        def _():
            gather1(g // per - 2)

        return 0

    lax.fori_loop(0, groups, attend, 0)
    for c in range(max(0, groups // (CHUNK // GROUP) - 2), chunks):
        gather1(c)

    gain_m = gm_ref[...].astype(F32)
    for c in range(chunks):
        for i in order:
            frm = peer(i)
            piece(hg.at[c, frm], hg.at[c, frm], g1s.at[c, frm], g1r.at[c, frm], frm).wait_recv()
        blocks = []
        part = jnp.zeros((CHUNK, 128), F32)
        for t in range(chips):
            block = jnp.concatenate([hg[c, CORES * t + k].astype(F32) for k in range(CORES)], 0)
            for u in range(cols // 128):
                sub = block[:, 128 * u:128 * (u + 1)]
                blocks.append(sub)
                part += sub * sub
        scale = lax.rsqrt(jnp.sum(part, -1, keepdims=True) / d + 1e-6)
        for j in range(tiles):
            a16[pl.ds(c * CHUNK, CHUNK), pl.ds(128 * j, 128)] = (blocks[j] * scale * gain_m[j:j + 1]).astype(BF16)

    load_wg.wait()
    load_wu.wait()
    width = 256

    def hidden(j, _):
        at = pl.ds(pl.multiple_of(j * width, width), width)
        b = a16[...]
        gate = jnp.dot(b, wg[:, at], preferred_element_type=F32)
        up = jnp.dot(b, wu[:, at], preferred_element_type=F32)
        hb[:, at] = (gate / (1.0 + jnp.exp(-gate)) * up).astype(BF16)
        return 0

    lax.fori_loop(0, ff // width, hidden, 0)
    load_wd.wait()

    far = [chips // 2]
    for i in range(chips // 2 - 1, 0, -1):
        far += [i, chips - i]
    far.append(0)

    for i in far:
        t = lax.rem(z + i, chips)
        term = jnp.dot(hb[...], wd[:, pl.ds(pl.multiple_of(t * cols, 128), cols)], preferred_element_type=F32)
        for k in range(CORES):
            to = CORES * t + k
            for c in range(chunks):
                send2[to, c] = term[c * CHUNK + half * k:c * CHUNK + half * (k + 1)].astype(BF16)
            if i:
                piece(send2.at[to], recv2.at[me], s2s.at[to], s2r.at[me], to).start()
    other = CORES * z + (CORES - 1 - core)
    piece(send2.at[other], recv2.at[me], s2s.at[other], s2r.at[me], other).start()

    for i in order:
        frm = peer(i)
        piece(send2.at[frm], recv2.at[frm], s2s.at[frm], s2r.at[frm], frm).wait_recv()
    for c in range(chunks):
        total = send2[me, c].astype(F32)
        for i in order:
            total += recv2[peer(i), c].astype(F32)
        yg[me, c] = (hg[c, me].astype(F32) + total).astype(BF16)
    for i in order:
        to = peer(i)
        piece(yg.at[me], yg.at[me], g2s.at[to], g2r.at[me], to).start()
    for i in order:
        frm = peer(i)
        piece(yg.at[frm], yg.at[frm], g2s.at[frm], g2r.at[frm], frm).wait_recv()
    for c in range(chunks):
        for t in range(chips):
            both = jnp.concatenate([yg[CORES * t + k, c].astype(F32) for k in range(CORES)], 0)
            out_ref[pl.ds(c * CHUNK, CHUNK), pl.ds(t * cols, cols)] = both.astype(BF16)

    for i in order:
        to = peer(i)
        for c in range(chunks):
            piece(send1.at[c, to], recv1.at[c, me], s1s.at[c, to], s1r.at[c, me], to).wait_send()
            piece(hg.at[c, me], hg.at[c, me], g1s.at[c, to], g1r.at[c, me], to).wait_send()
        piece(send2.at[to], recv2.at[me], s2s.at[to], s2r.at[me], to).wait_send()
        piece(yg.at[me], yg.at[me], g2s.at[to], g2r.at[me], to).wait_send()


def solution(mesh):
    n = mesh.shape["tp"]

    def step(x, k_cache, v_cache, gain_a, wq, wo, gain_m, w_gate, w_up, w_down):
        rows, d = x.shape
        cache = k_cache.shape[1]
        ff = w_gate.shape[1]
        k_cache, v_cache = k_cache.reshape(rows, cache, HEAD), v_cache.reshape(rows, cache, HEAD)
        chunks, half, cols = rows // CHUNK, CHUNK // CORES, d // (n // CORES)
        trig = jnp.asarray(rotary_table(cache, HEAD // 2))
        any_, vmem = pl.BlockSpec(memory_space=pl.ANY), pl.BlockSpec(memory_space=pltpu.VMEM)
        dma = pltpu.SemaphoreType.DMA
        return pl.pallas_call(
            functools.partial(layer, n),
            name="layer",
            out_shape=jax.ShapeDtypeStruct((rows, d), BF16),
            in_specs=[any_, any_, any_, vmem, vmem, any_, any_, vmem, any_, any_, any_],
            out_specs=vmem,
            scratch_shapes=[
                pltpu.VMEM((rows, d), BF16),
                pltpu.VMEM((rows, d), F32),
                pltpu.VMEM((rows, d), BF16),
                pltpu.VMEM(wq.shape, BF16),
                pltpu.VMEM(wo.shape, BF16),
                pltpu.VMEM(w_gate.shape, BF16),
                pltpu.VMEM(w_up.shape, BF16),
                pltpu.VMEM(w_down.shape, BF16),
                pltpu.VMEM((SLOTS, GROUP, cache, HEAD), BF16),
                pltpu.VMEM((SLOTS, GROUP, cache, HEAD), BF16),
                pltpu.VMEM((rows, HEAD), F32),
                pltpu.VMEM((rows, HEAD), F32),
                pltpu.VMEM((rows, ff), BF16),
                pltpu.VMEM((chunks, n, half, cols), BF16),
                pltpu.VMEM((chunks, n, half, cols), BF16),
                pltpu.VMEM((chunks, n, half, cols), BF16),
                pltpu.VMEM((n, chunks, half, cols), BF16),
                pltpu.VMEM((n, chunks, half, cols), BF16),
                pltpu.VMEM((n, chunks, half, cols), BF16),
                dma((6,)),
                dma((SLOTS,)),
                dma((SLOTS,)),
                dma((chunks, n)),
                dma((chunks, n)),
                dma((chunks, n)),
                dma((chunks, n)),
                dma((n,)),
                dma((n,)),
                dma((n,)),
                dma((n,)),
            ],
            compiler_params=pltpu.CompilerParams(
                collective_id=0, has_side_effects=True, vmem_limit_bytes=67_043_328
            ),
        )(x, k_cache, v_cache, gain_a.reshape(-1, 128), trig, wq, wo, gain_m.reshape(-1, 128), w_gate, w_up, w_down)

    states, cache, columns, rows_of = P("dp", None), P("dp", None, "tp", None), P(None, "tp"), P("tp", None)
    return jax.shard_map(
        step,
        mesh=mesh,
        in_specs=(states, cache, cache, P(None), columns, rows_of, P(None), columns, columns, rows_of),
        out_specs=states,
        check_vma=False,
    )
```

time: 279 us -> 83.3 us (0.30)
  waiting for transfers between devices: 213 us -> 0 us
  Pallas kernels: 0 us -> 81.4 us
  matrix products: 46.6 us -> 0 us
  between operations: 13.5 us -> 0.01 us
  other arithmetic: 5.66 us -> 0 us
    psum x2 -> x0, waiting for transfers between devices: 213 us -> none  [added(): lax.psum(term.astype(jnp.bfloat16), 'tp').astype(jnp.float32)]
    pallas_call x0 -> x1, Pallas kernels: none -> 81.4 us  [step(): pl.pallas_call(functools.partial(layer, n), name='layer', out_shape=jax.S...]
    dot_general x6 -> x0, matrix products: 46.6 us -> none  [the longest x2 27.4 us: einsum(): return jnp.einsum(form, a.astype(jnp.float32), b.astype(jnp.float32))]
  transfers between devices with their start and end apart: 2 -> 0, of which waited for: 2 -> 0; matrix products, arithmetic and copies ran while one was open for 0% -> 0% of each run, Pallas kernels for 0% -> 0%
where the time goes in v1:
time: 83.3 us; the launch traced here: 83.1 us
  Pallas kernels  81.4 us (98%)
  local copies, waits for them, and re-layouts  1.77 us (2%)
    pallas_call x1, Pallas kernels, step(): pl.pallas_call(functools.partial(layer, n), name='layer', out_shape=jax.S...  81.4 us
    unnamed x1, local copies, waits for them, and re-layouts  1.77 us

profile of v1, /device:TPU:21, one launch (start us, length us, event | category | flops | bytes accessed | tf_op | source)
XLA Modules:
  0.0 83.1 jit_solution(15910121834437095989)
XLA Ops:
  0.0 81.4 %layer.1 = bf16[64,3072]{1,0:T(8,128)(2,1)} custom-call(bf16[64,3072]{1,0:T(8,128)(2,1)} %x_hbm.1, bf16[64,1024,256]{2,1,0:T(8,128)(2,1)} %bitcast.4, bf16[64,1024,256]{2,1,0:T(8,128)(2,1)} %bitcast.5, bf16[24,128]{1,0:T(8,128)(2,1)} %bitcast.6, f32[2,128]{1,0:T(2,128)} %constant.2.clone.trig_ref, bf16[3072,256]{1,0:T(8,128)(2,1)} %wq_hbm.1, ...), custom_call_target="tpu_custom_call" | custom-call | tf_op jit(solution)/shard_map/layer/pallas_call | solution.py:266
  81.4 1.8 %copy.13 = bf16[64,3072]{1,0:T(8,128)(2,1)} copy(bf16[64,3072]{1,0:T(8,128)(2,1)} %layer.1) | data formatting | bytes 786432

commit v2 on v1

--- a/solution.py
+++ b/solution.py
@@ -123,11 +123,15 @@
         at = pl.ds(pl.multiple_of(g * GROUP, GROUP), GROUP)
         load_k(g).wait()
         qg = q32[at, :]
-        scores = None
-        for i in range(GROUP):
-            mine = jnp.where(line == i, qg, 0.0).astype(BF16)
-            s = lax.dot_general(mine, kbuf[slot, i], (((1,), (1,)), ((), ())), preferred_element_type=F32)
-            scores = s if scores is None else scores + s
+        lhs = [jnp.where(line == i, qg, 0.0).astype(BF16) for i in range(GROUP)]
+        scores = []
+        for j in range(kbuf.shape[2] // 256):
+            total = None
+            for i in range(GROUP):
+                s = lax.dot_general(lhs[i], kbuf[slot, i, pl.ds(256 * j, 256)], (((1,), (1,)), ((), ())), preferred_element_type=F32)
+                total = s if total is None else total + s
+            scores.append(total)
+        scores = jnp.concatenate(scores, 1)
 
         @pl.when(g + SLOTS < groups)
         def _():
@@ -137,12 +141,13 @@
         e = jnp.exp(scores - jnp.max(scores, -1, keepdims=True))
         w = e * (1.0 / jnp.sum(e, -1, keepdims=True))
         load_v(g).wait()
-        seen = None
-        for i in range(GROUP):
-            mine = jnp.where(line == i, w, 0.0).astype(BF16)
-            s = jnp.dot(mine, vbuf[slot, i], preferred_element_type=F32)
-            seen = s if seen is None else seen + s
-        s32[at, :] = seen
+        lhs = [jnp.where(line == i, w, 0.0).astype(BF16) for i in range(GROUP)]
+        for j in range(HEAD // 128):
+            total = None
+            for i in range(GROUP):
+                s = jnp.dot(lhs[i], vbuf[slot, i, :, pl.ds(128 * j, 128)], preferred_element_type=F32)
+                total = s if total is None else total + s
+            s32[at, pl.ds(128 * j, 128)] = total
 
         @pl.when(g + SLOTS < groups)
         def _():
@@ -203,26 +208,30 @@
         hb[:, at] = (gate / (1.0 + jnp.exp(-gate)) * up).astype(BF16)
         return 0
 
-    lax.fori_loop(0, ff // width, hidden, 0)
+    lax.fori_loop(0, ff // width, hidden, 0, unroll=2)
     load_wd.wait()
 
-    far = [chips // 2]
-    for i in range(chips // 2 - 1, 0, -1):
-        far += [i, chips - i]
-    far.append(0)
-
-    for i in far:
-        t = lax.rem(z + i, chips)
-        term = jnp.dot(hb[...], wd[:, pl.ds(pl.multiple_of(t * cols, 128), cols)], preferred_element_type=F32)
-        for k in range(CORES):
-            to = CORES * t + k
-            for c in range(chunks):
-                send2[to, c] = term[c * CHUNK + half * k:c * CHUNK + half * (k + 1)].astype(BF16)
-            if i:
+    pair = 2 * cols
+    pairs = chips // 2
+    for i in (pairs // 2, pairs // 2 - 1, pairs - 1, 0):
+        p = lax.rem(z // 2 + i, pairs)
+        b = hb[...]
+        terms = []
+        for u in range(pair // width):
+            at = pl.ds(pl.multiple_of(p * pair + u * width, width), width)
+            terms.append(jnp.dot(b, wd[:, at], preferred_element_type=F32))
+        term = jnp.concatenate(terms, 1)
+        for t in range(2):
+            for k in range(CORES):
+                for c in range(chunks):
+                    row = c * CHUNK + half * k
+                    send2[2 * CORES * p + CORES * t + k, c] = term[row:row + half, t * cols:(t + 1) * cols].astype(BF16)
+        for t in range(2 * CORES):
+            to = 2 * CORES * p + t
+
+            @pl.when(to != me)
+            def _():
                 piece(send2.at[to], recv2.at[me], s2s.at[to], s2r.at[me], to).start()
-    other = CORES * z + (CORES - 1 - core)
-    piece(send2.at[other], recv2.at[me], s2s.at[other], s2r.at[me], other).start()
-
     for i in order:
         frm = peer(i)
         piece(send2.at[frm], recv2.at[frm], s2s.at[frm], s2r.at[frm], frm).wait_recv()

time: 83.3 us -> 80.5 us (0.966)
  Pallas kernels: 81.4 us -> 78.4 us
    pallas_call x1, Pallas kernels: 81.4 us -> 78.4 us  [step(): pl.pallas_call(functools.partial(layer, n), name='layer', out_shape=jax.S...]
where the time goes in v2:
time: 80.5 us; the launch traced here: 80.2 us
  Pallas kernels  78.4 us (97%)
  local copies, waits for them, and re-layouts  1.77 us (2%)
    pallas_call x1, Pallas kernels, step(): pl.pallas_call(functools.partial(layer, n), name='layer', out_shape=jax.S...  78.4 us
    unnamed x1, local copies, waits for them, and re-layouts  1.77 us

profile of v2, /device:TPU:21, one launch (start us, length us, event | category | flops | bytes accessed | tf_op | source)
XLA Modules:
  0.0 80.2 jit_solution(2711503197718592061)
XLA Ops:
  0.0 78.4 %layer.1 = bf16[64,3072]{1,0:T(8,128)(2,1)} custom-call(bf16[64,3072]{1,0:T(8,128)(2,1)} %x_hbm.1, bf16[64,1024,256]{2,1,0:T(8,128)(2,1)} %bitcast.4, bf16[64,1024,256]{2,1,0:T(8,128)(2,1)} %bitcast.5, bf16[24,128]{1,0:T(8,128)(2,1)} %bitcast.6, f32[2,128]{1,0:T(2,128)} %constant.2.clone.trig_ref, bf16[3072,256]{1,0:T(8,128)(2,1)} %wq_hbm.1, ...), custom_call_target="tpu_custom_call" | custom-call | tf_op jit(solution)/shard_map/layer/pallas_call | solution.py:275
  78.4 1.8 %copy.13 = bf16[64,3072]{1,0:T(8,128)(2,1)} copy(bf16[64,3072]{1,0:T(8,128)(2,1)} %layer.1) | data formatting | bytes 786432

commit v3 on v2

--- a/solution.py
+++ b/solution.py
@@ -14,6 +14,8 @@
 GROUP = 8
 CHUNK = 16
 SLOTS = 3
+LATE = 1
+UNROLL = 2
 MESH = pl.DeviceIdType.MESH
 F32, BF16 = jnp.float32, jnp.bfloat16
 
@@ -24,8 +26,8 @@
 
 
 def layer(n, x_hbm, k_hbm, v_hbm, ga_ref, trig_ref, wq_hbm, wo_hbm, gm_ref, wg_hbm, wu_hbm, wd_hbm, out_ref,
-          x16, xs, a16, wq, wo, wg, wu, wd, kbuf, vbuf, q32, s32, hb,
-          send1, recv1, hg, send2, recv2, yg,
+          x16, xs, a16, wq, wo, wg, wu, wd, kbuf, vbuf, q32, hb,
+          send1, recv1, hg, send2, recv2, yg, send3, recv3, yh,
           in_sem, k_sem, v_sem, s1s, s1r, g1s, g1r, s2s, s2r, g2s, g2r):
     rows, d = x16.shape
     ff = wg.shape[1]
@@ -41,6 +43,10 @@
         return lax.rem(me + i, n)
 
     order = sorted(range(1, n), key=lambda i: -min(i, n - i))
+    far = [chips // 2]
+    for i in range(chips // 2 - 1, 0, -1):
+        far += [i, chips - i]
+    far.append(0)
 
     load_x = pltpu.make_async_copy(x_hbm, x16, in_sem.at[0])
     load_wq = pltpu.make_async_copy(wq_hbm, wq, in_sem.at[1])
@@ -93,24 +99,30 @@
         return pltpu.make_async_remote_copy(src_ref=src, dst_ref=dst, send_sem=ssem, recv_sem=rsem,
                                             device_id={"tp": to}, device_id_type=MESH)
 
-    def scatter1(c):
-        seen = s32[pl.ds(pl.multiple_of(c * CHUNK, CHUNK), CHUNK), :].astype(BF16)
+    def scatter1(u, seen):
         for t in range(chips):
             term = jnp.dot(seen, wo[:, pl.ds(t * cols, cols)], preferred_element_type=F32)
-            for k in range(CORES):
-                send1[c, CORES * t + k] = term[half * k:half * (k + 1)].astype(BF16)
-        for i in order:
-            to = peer(i)
-            piece(send1.at[c, to], recv1.at[c, me], s1s.at[c, to], s1r.at[c, me], to).start()
+            send1[u, t] = term.astype(BF16)
+        kind = lax.rem(u, CORES)
+        c = u // CORES
+        for i in far:
+            t = lax.rem(z + i, chips)
+            to = CORES * t + kind
+            copy = piece(send1.at[u, t], recv1.at[c, me], s1s.at[u, t], s1r.at[c, me], to)
+            if i:
+                copy.start()
+            else:
+                pl.when(core != kind)(copy.start)
 
     def gather1(c):
-        total = send1[c, me].astype(F32)
+        u = CORES * c + core
+        total = send1[u, z].astype(F32)
         for i in order:
             frm = peer(i)
-            piece(send1.at[c, frm], recv1.at[c, frm], s1s.at[c, frm], s1r.at[c, frm], frm).wait_recv()
+            piece(send1.at[u, z], recv1.at[c, frm], s1s.at[u, z], s1r.at[c, frm], frm).wait_recv()
         for i in order:
             total += recv1[c, peer(i)].astype(F32)
-        at = pl.ds(pl.multiple_of(c * CHUNK + core * half, half), half)
+        at = pl.ds(pl.multiple_of(u * half, half), half)
         hg[c, me] = (xs[at, pl.ds(pl.multiple_of(z * cols, 128), cols)] + total).astype(BF16)
         for i in order:
             to = peer(i)
@@ -142,12 +154,14 @@
         w = e * (1.0 / jnp.sum(e, -1, keepdims=True))
         load_v(g).wait()
         lhs = [jnp.where(line == i, w, 0.0).astype(BF16) for i in range(GROUP)]
+        seen = []
         for j in range(HEAD // 128):
             total = None
             for i in range(GROUP):
                 s = jnp.dot(lhs[i], vbuf[slot, i, :, pl.ds(128 * j, 128)], preferred_element_type=F32)
                 total = s if total is None else total + s
-            s32[at, pl.ds(128 * j, 128)] = total
+            seen.append(total)
+        seen = jnp.concatenate(seen, 1).astype(BF16)
 
         @pl.when(g + SLOTS < groups)
         def _():
@@ -159,105 +173,127 @@
             load_wu.start()
             load_wd.start()
 
-        @pl.when(g == 1)
+        @pl.when(g == 0)
         def _():
             load_wo.wait()
 
-        per = CHUNK // GROUP
-
-        @pl.when(lax.rem(g, per) == per - 1)
-        def _():
-            scatter1(g // per)
-
-        @pl.when((lax.rem(g, per) == 0) & (g >= 2 * per))
-        def _():
-            gather1(g // per - 2)
+        scatter1(g, seen)
+
+        @pl.when((lax.rem(g, CORES) == 0) & (g >= 2 * CORES))
+        def _():
+            gather1(g // CORES - 2)
 
         return 0
 
     lax.fori_loop(0, groups, attend, 0)
-    for c in range(max(0, groups // (CHUNK // GROUP) - 2), chunks):
+    for c in range(chunks - 2, chunks):
         gather1(c)
 
     gain_m = gm_ref[...].astype(F32)
-    for c in range(chunks):
-        for i in order:
-            frm = peer(i)
-            piece(hg.at[c, frm], hg.at[c, frm], g1s.at[c, frm], g1r.at[c, frm], frm).wait_recv()
-        blocks = []
-        part = jnp.zeros((CHUNK, 128), F32)
-        for t in range(chips):
-            block = jnp.concatenate([hg[c, CORES * t + k].astype(F32) for k in range(CORES)], 0)
-            for u in range(cols // 128):
-                sub = block[:, 128 * u:128 * (u + 1)]
-                blocks.append(sub)
-                part += sub * sub
-        scale = lax.rsqrt(jnp.sum(part, -1, keepdims=True) / d + 1e-6)
-        for j in range(tiles):
-            a16[pl.ds(c * CHUNK, CHUNK), pl.ds(128 * j, 128)] = (blocks[j] * scale * gain_m[j:j + 1]).astype(BF16)
-
-    load_wg.wait()
-    load_wu.wait()
     width = 256
-
-    def hidden(j, _):
-        at = pl.ds(pl.multiple_of(j * width, width), width)
-        b = a16[...]
-        gate = jnp.dot(b, wg[:, at], preferred_element_type=F32)
-        up = jnp.dot(b, wu[:, at], preferred_element_type=F32)
-        hb[:, at] = (gate / (1.0 + jnp.exp(-gate)) * up).astype(BF16)
-        return 0
-
-    lax.fori_loop(0, ff // width, hidden, 0, unroll=2)
-    load_wd.wait()
-
     pair = 2 * cols
     pairs = chips // 2
-    for i in (pairs // 2, pairs // 2 - 1, pairs - 1, 0):
-        p = lax.rem(z // 2 + i, pairs)
-        b = hb[...]
-        terms = []
-        for u in range(pair // width):
-            at = pl.ds(pl.multiple_of(p * pair + u * width, width), width)
-            terms.append(jnp.dot(b, wd[:, at], preferred_element_type=F32))
-        term = jnp.concatenate(terms, 1)
-        for t in range(2):
-            for k in range(CORES):
-                for c in range(chunks):
-                    row = c * CHUNK + half * k
-                    send2[2 * CORES * p + CORES * t + k, c] = term[row:row + half, t * cols:(t + 1) * cols].astype(BF16)
-        for t in range(2 * CORES):
-            to = 2 * CORES * p + t
-
-            @pl.when(to != me)
-            def _():
-                piece(send2.at[to], recv2.at[me], s2s.at[to], s2r.at[me], to).start()
-    for i in order:
-        frm = peer(i)
-        piece(send2.at[frm], recv2.at[frm], s2s.at[frm], s2r.at[frm], frm).wait_recv()
-    for c in range(chunks):
-        total = send2[me, c].astype(F32)
-        for i in order:
-            total += recv2[peer(i), c].astype(F32)
-        yg[me, c] = (hg[c, me].astype(F32) + total).astype(BF16)
-    for i in order:
-        to = peer(i)
-        piece(yg.at[me], yg.at[me], g2s.at[to], g2r.at[me], to).start()
-    for i in order:
-        frm = peer(i)
-        piece(yg.at[frm], yg.at[frm], g2s.at[frm], g2r.at[frm], frm).wait_recv()
-    for c in range(chunks):
-        for t in range(chips):
-            both = jnp.concatenate([yg[CORES * t + k, c].astype(F32) for k in range(CORES)], 0)
-            out_ref[pl.ds(c * CHUNK, CHUNK), pl.ds(t * cols, cols)] = both.astype(BF16)
+
+    def mlp(first, count, send, recv, ssem, rsem):
+        for c in range(first, first + count):
+            for i in order:
+                frm = peer(i)
+                piece(hg.at[c, frm], hg.at[c, frm], g1s.at[c, frm], g1r.at[c, frm], frm).wait_recv()
+            blocks = []
+            part = jnp.zeros((CHUNK, 128), F32)
+            for t in range(chips):
+                block = jnp.concatenate([hg[c, CORES * t + k].astype(F32) for k in range(CORES)], 0)
+                for u in range(cols // 128):
+                    sub = block[:, 128 * u:128 * (u + 1)]
+                    blocks.append(sub)
+                    part += sub * sub
+            scale = lax.rsqrt(jnp.sum(part, -1, keepdims=True) / d + 1e-6)
+            for j in range(tiles):
+                a16[pl.ds(c * CHUNK, CHUNK), pl.ds(128 * j, 128)] = (blocks[j] * scale * gain_m[j:j + 1]).astype(BF16)
+
+        mine = pl.ds(first * CHUNK, count * CHUNK)
+        if first == 0:
+            load_wg.wait()
+            load_wu.wait()
+
+        def hidden(j, _):
+            at = pl.ds(pl.multiple_of(j * width, width), width)
+            b = a16[mine, :]
+            gate = jnp.dot(b, wg[:, at], preferred_element_type=F32)
+            up = jnp.dot(b, wu[:, at], preferred_element_type=F32)
+            hb[mine, at] = (gate / (1.0 + jnp.exp(-gate)) * up).astype(BF16)
+            return 0
+
+        lax.fori_loop(0, ff // width, hidden, 0, unroll=UNROLL)
+        if first == 0:
+            load_wd.wait()
+
+        for i in (pairs // 2, pairs // 2 - 1, pairs - 1, 0):
+            p = lax.rem(z // 2 + i, pairs)
+            b = hb[mine, :]
+            terms = []
+            for o in range(0, pair, width):
+                at = pl.ds(pl.multiple_of(p * pair + o, 128), width)
+                terms.append(jnp.dot(b, wd[:, at], preferred_element_type=F32))
+            term = jnp.concatenate(terms, 1)
+            for t in range(2):
+                for k in range(CORES):
+                    for c in range(count):
+                        row = c * CHUNK + half * k
+                        send[2 * CORES * p + CORES * t + k, c] = term[row:row + half, t * cols:(t + 1) * cols].astype(BF16)
+            for t in range(2 * CORES):
+                to = 2 * CORES * p + t
+                copy = piece(send.at[to], recv.at[me], ssem.at[to], rsem.at[me], to)
+                if i:
+                    copy.start()
+                else:
+                    pl.when(to != me)(copy.start)
+
+    def gather2(first, count, send, recv, ssem, rsem, y, gsem, grsem):
+        for i in order:
+            frm = peer(i)
+            piece(send.at[frm], recv.at[frm], ssem.at[frm], rsem.at[frm], frm).wait_recv()
+        for c in range(count):
+            total = send[me, c].astype(F32)
+            for i in order:
+                total += recv[peer(i), c].astype(F32)
+            y[me, c] = (hg[first + c, me].astype(F32) + total).astype(BF16)
+        for i in order:
+            to = peer(i)
+            piece(y.at[me], y.at[me], gsem.at[to], grsem.at[me], to).start()
+
+    def collect2(first, count, y, gsem, grsem):
+        for i in order:
+            frm = peer(i)
+            piece(y.at[frm], y.at[frm], gsem.at[frm], grsem.at[frm], frm).wait_recv()
+        for c in range(count):
+            for t in range(chips):
+                both = jnp.concatenate([y[CORES * t + k, c].astype(F32) for k in range(CORES)], 0)
+                out_ref[pl.ds((first + c) * CHUNK, CHUNK), pl.ds(t * cols, cols)] = both.astype(BF16)
+
+    early = chunks - LATE
+    mlp(0, early, send2, recv2, s2s.at[0], s2r.at[0])
+    mlp(early, LATE, send3, recv3, s2s.at[1], s2r.at[1])
+    gather2(0, early, send2, recv2, s2s.at[0], s2r.at[0], yg, g2s.at[0], g2r.at[0])
+    gather2(early, LATE, send3, recv3, s2s.at[1], s2r.at[1], yh, g2s.at[1], g2r.at[1])
+    collect2(0, early, yg, g2s.at[0], g2r.at[0])
+    collect2(early, LATE, yh, g2s.at[1], g2r.at[1])
 
     for i in order:
         to = peer(i)
         for c in range(chunks):
-            piece(send1.at[c, to], recv1.at[c, me], s1s.at[c, to], s1r.at[c, me], to).wait_send()
             piece(hg.at[c, me], hg.at[c, me], g1s.at[c, to], g1r.at[c, me], to).wait_send()
-        piece(send2.at[to], recv2.at[me], s2s.at[to], s2r.at[me], to).wait_send()
-        piece(yg.at[me], yg.at[me], g2s.at[to], g2r.at[me], to).wait_send()
+        for at, send, y in ((0, send2, yg), (1, send3, yh)):
+            piece(send.at[to], send.at[to], s2s.at[at, to], s2r.at[at, me], to).wait_send()
+            piece(y.at[me], y.at[me], g2s.at[at, to], g2r.at[at, me], to).wait_send()
+    for u in range(groups):
+        for i in far:
+            t = lax.rem(z + i, chips)
+            copy = piece(send1.at[u, t], send1.at[u, t], s1s.at[u, t], s1r.at[u // CORES, me], me)
+            if i:
+                copy.wait_send()
+            else:
+                pl.when(core != u % CORES)(copy.wait_send)
 
 
 def solution(mesh):
@@ -290,25 +326,23 @@
                 pltpu.VMEM((SLOTS, GROUP, cache, HEAD), BF16),
                 pltpu.VMEM((SLOTS, GROUP, cache, HEAD), BF16),
                 pltpu.VMEM((rows, HEAD), F32),
-                pltpu.VMEM((rows, HEAD), F32),
                 pltpu.VMEM((rows, ff), BF16),
+                pltpu.VMEM((rows // GROUP, n // CORES, half, cols), BF16),
                 pltpu.VMEM((chunks, n, half, cols), BF16),
                 pltpu.VMEM((chunks, n, half, cols), BF16),
-                pltpu.VMEM((chunks, n, half, cols), BF16),
-                pltpu.VMEM((n, chunks, half, cols), BF16),
-                pltpu.VMEM((n, chunks, half, cols), BF16),
-                pltpu.VMEM((n, chunks, half, cols), BF16),
+                *[pltpu.VMEM((n, chunks - LATE, half, cols), BF16)] * 3,
+                *[pltpu.VMEM((n, LATE, half, cols), BF16)] * 3,
                 dma((6,)),
                 dma((SLOTS,)),
                 dma((SLOTS,)),
+                dma((rows // GROUP, n // CORES)),
                 dma((chunks, n)),
                 dma((chunks, n)),
                 dma((chunks, n)),
-                dma((chunks, n)),
-                dma((n,)),
-                dma((n,)),
-                dma((n,)),
-                dma((n,)),
+                dma((2, n)),
+                dma((2, n)),
+                dma((2, n)),
+                dma((2, n)),
             ],
             compiler_params=pltpu.CompilerParams(
                 collective_id=0, has_side_effects=True, vmem_limit_bytes=67_043_328

time: 80.5 us -> 75.6 us (0.939); the launches traced: 80.2 us -> 74.4 us
  Pallas kernels: 78.4 us -> 72.6 us
    pallas_call x1, Pallas kernels: 78.4 us -> 72.6 us  [step(): pl.pallas_call(functools.partial(layer, n), name='layer', out_shape=jax.S...]
where the time goes in v3:
time: 75.6 us; the launch traced here: 74.4 us
  Pallas kernels  72.6 us (96%)
  local copies, waits for them, and re-layouts  1.77 us (2%)
    pallas_call x1, Pallas kernels, step(): pl.pallas_call(functools.partial(layer, n), name='layer', out_shape=jax.S...  72.6 us
    unnamed x1, local copies, waits for them, and re-layouts  1.77 us

profile of v3, /device:TPU:21, one launch (start us, length us, event | category | flops | bytes accessed | tf_op | source)
XLA Modules:
  0.0 74.4 jit_solution(7604895269531081601)
XLA Ops:
  0.0 72.6 %layer.1 = bf16[64,3072]{1,0:T(8,128)(2,1)} custom-call(bf16[64,3072]{1,0:T(8,128)(2,1)} %x_hbm.1, bf16[64,1024,256]{2,1,0:T(8,128)(2,1)} %bitcast.4, bf16[64,1024,256]{2,1,0:T(8,128)(2,1)} %bitcast.5, bf16[24,128]{1,0:T(8,128)(2,1)} %bitcast.6, f32[2,128]{1,0:T(2,128)} %constant.2.clone.trig_ref, bf16[3072,256]{1,0:T(8,128)(2,1)} %wq_hbm.1, ...), custom_call_target="tpu_custom_call" | custom-call | tf_op jit(solution)/shard_map/layer/pallas_call | solution.py:311
  72.7 1.8 %copy.13 = bf16[64,3072]{1,0:T(8,128)(2,1)} copy(bf16[64,3072]{1,0:T(8,128)(2,1)} %layer.1) | data formatting | bytes 786432

commit v4 on v3

--- a/solution.py
+++ b/solution.py
@@ -15,7 +15,7 @@
 CHUNK = 16
 SLOTS = 3
 LATE = 1
-UNROLL = 2
+UNROLL = True
 MESH = pl.DeviceIdType.MESH
 F32, BF16 = jnp.float32, jnp.bfloat16
 
@@ -27,8 +27,8 @@
 
 def layer(n, x_hbm, k_hbm, v_hbm, ga_ref, trig_ref, wq_hbm, wo_hbm, gm_ref, wg_hbm, wu_hbm, wd_hbm, out_ref,
           x16, xs, a16, wq, wo, wg, wu, wd, kbuf, vbuf, q32, hb,
-          send1, recv1, hg, send2, recv2, yg, send3, recv3, yh,
-          in_sem, k_sem, v_sem, s1s, s1r, g1s, g1r, s2s, s2r, g2s, g2r):
+          send1, recv1, hg, xs2, xr2, sz, rz, yg, send3, recv3, yh,
+          in_sem, k_sem, v_sem, s1s, s1r, g1s, g1r, s2s, s2r, g2s, g2r, xss, xsr, zs, zr, ys, yr, fs, fr):
     rows, d = x16.shape
     ff = wg.shape[1]
     groups, chunks = rows // GROUP, rows // CHUNK
@@ -99,10 +99,12 @@
         return pltpu.make_async_remote_copy(src_ref=src, dst_ref=dst, send_sem=ssem, recv_sem=rsem,
                                             device_id={"tp": to}, device_id_type=MESH)
 
-    def scatter1(u, seen):
+    def term1(u, seen):
+        term = jnp.concatenate([jnp.dot(seen, wo[:, pl.ds(o, 256)], preferred_element_type=F32) for o in range(0, d, 256)], 1)
         for t in range(chips):
-            term = jnp.dot(seen, wo[:, pl.ds(t * cols, cols)], preferred_element_type=F32)
-            send1[u, t] = term.astype(BF16)
+            send1[u, t] = term[:, t * cols:(t + 1) * cols].astype(BF16)
+
+    def scatter1(u):
         kind = lax.rem(u, CORES)
         c = u // CORES
         for i in far:
@@ -130,42 +132,47 @@
 
     line = lax.broadcasted_iota(jnp.int32, (GROUP, 1), 0)
 
-    def attend(g, _):
+    def scores_of(g):
         slot = lax.rem(g, SLOTS)
-        at = pl.ds(pl.multiple_of(g * GROUP, GROUP), GROUP)
-        load_k(g).wait()
-        qg = q32[at, :]
+        qg = q32[pl.ds(pl.multiple_of(g * GROUP, GROUP), GROUP), :]
         lhs = [jnp.where(line == i, qg, 0.0).astype(BF16) for i in range(GROUP)]
-        scores = []
+        out = []
         for j in range(kbuf.shape[2] // 256):
             total = None
             for i in range(GROUP):
                 s = lax.dot_general(lhs[i], kbuf[slot, i, pl.ds(256 * j, 256)], (((1,), (1,)), ((), ())), preferred_element_type=F32)
                 total = s if total is None else total + s
-            scores.append(total)
-        scores = jnp.concatenate(scores, 1)
-
-        @pl.when(g + SLOTS < groups)
-        def _():
-            load_k(g + SLOTS).start()
-
-        scores = scores * HEAD**-0.5
+            out.append(total)
+        return jnp.concatenate(out, 1) * HEAD**-0.5
+
+    def seen_of(g, scores):
+        slot = lax.rem(g, SLOTS)
         e = jnp.exp(scores - jnp.max(scores, -1, keepdims=True))
         w = e * (1.0 / jnp.sum(e, -1, keepdims=True))
-        load_v(g).wait()
         lhs = [jnp.where(line == i, w, 0.0).astype(BF16) for i in range(GROUP)]
-        seen = []
+        out = []
         for j in range(HEAD // 128):
             total = None
             for i in range(GROUP):
                 s = jnp.dot(lhs[i], vbuf[slot, i, :, pl.ds(128 * j, 128)], preferred_element_type=F32)
                 total = s if total is None else total + s
-            seen.append(total)
-        seen = jnp.concatenate(seen, 1).astype(BF16)
+            out.append(total)
+        return jnp.concatenate(out, 1).astype(BF16)
+
+    def attend(g, scores):
+        load_v(g).wait()
+        load_k(g + 1).wait()
+        later = scores_of(g + 1)
+        seen = seen_of(g, scores)
+        term1(g, seen)
 
         @pl.when(g + SLOTS < groups)
         def _():
             load_v(g + SLOTS).start()
+
+        @pl.when(g + 1 + SLOTS < groups)
+        def _():
+            load_k(g + 1 + SLOTS).start()
 
         @pl.when(g == groups - SLOTS - 1)
         def _():
@@ -173,19 +180,22 @@
             load_wu.start()
             load_wd.start()
 
-        @pl.when(g == 0)
-        def _():
-            load_wo.wait()
-
-        scatter1(g, seen)
+        scatter1(g)
 
         @pl.when((lax.rem(g, CORES) == 0) & (g >= 2 * CORES))
         def _():
             gather1(g // CORES - 2)
 
-        return 0
-
-    lax.fori_loop(0, groups, attend, 0)
+        return later
+
+    load_k(0).wait()
+    scores = scores_of(0)
+    load_k(SLOTS).start()
+    load_wo.wait()
+    scores = lax.fori_loop(0, groups - 1, attend, scores)
+    load_v(groups - 1).wait()
+    term1(groups - 1, seen_of(groups - 1, scores))
+    scatter1(groups - 1)
     for c in range(chunks - 2, chunks):
         gather1(c)
 
@@ -194,7 +204,11 @@
     pair = 2 * cols
     pairs = chips // 2
 
-    def mlp(first, count, send, recv, ssem, rsem):
+    early = chunks - LATE
+    far_pairs = ((pairs // 2, 1), (pairs - 1, 0)) if pairs > 2 else ((1,), (0,))
+    partner = CORES * z + 1 - core
+
+    def mlp(first, count, send):
         for c in range(first, first + count):
             for i in order:
                 frm = peer(i)
@@ -228,26 +242,91 @@
         if first == 0:
             load_wd.wait()
 
-        for i in (pairs // 2, pairs // 2 - 1, pairs - 1, 0):
-            p = lax.rem(z // 2 + i, pairs)
-            b = hb[mine, :]
-            terms = []
-            for o in range(0, pair, width):
-                at = pl.ds(pl.multiple_of(p * pair + o, 128), width)
-                terms.append(jnp.dot(b, wd[:, at], preferred_element_type=F32))
-            term = jnp.concatenate(terms, 1)
+        b = hb[mine, :]
+        for h in range(2):
+            blocks = [(lax.rem(z // 2 + i, pairs), i) for i in far_pairs[h]]
+            terms = [[jnp.dot(b, wd[:, pl.ds(pl.multiple_of(p * pair + o, 128), width)], preferred_element_type=F32)
+                      for o in range(0, pair, width)] for p, i in blocks]
+            send(h, blocks, [jnp.concatenate(t, 1).astype(BF16) for t in terms])
+
+    def unit(term, c, k, t):
+        row = c * CHUNK + half * k
+        return term[row:row + half, t * cols:(t + 1) * cols]
+
+    def scatter_late(h, blocks, terms):
+        for (p, i), term in zip(blocks, terms):
             for t in range(2):
                 for k in range(CORES):
-                    for c in range(count):
-                        row = c * CHUNK + half * k
-                        send[2 * CORES * p + CORES * t + k, c] = term[row:row + half, t * cols:(t + 1) * cols].astype(BF16)
+                    for c in range(LATE):
+                        send3[2 * CORES * p + CORES * t + k, c] = unit(term, c, k, t)
+        for p, i in blocks:
             for t in range(2 * CORES):
                 to = 2 * CORES * p + t
-                copy = piece(send.at[to], recv.at[me], ssem.at[to], rsem.at[me], to)
+                copy = piece(send3.at[to], recv3.at[me], s2s.at[to], s2r.at[me], to)
                 if i:
                     copy.start()
                 else:
                     pl.when(to != me)(copy.start)
+
+    def swap(h):
+        return piece(xs2.at[h, 1 - core], xr2.at[h], xss.at[h], xsr.at[h], partner)
+
+    def scatter_early(h, blocks, terms):
+        for b, term in enumerate(terms):
+            for t in range(2):
+                for k in range(CORES):
+                    for c in range(early):
+                        xs2[h, k, 2 * b + t, c] = unit(term, c, k, t)
+        swap(h).start()
+
+    def chip_piece(h, j, t):
+        return piece(sz.at[h, j], rz.at[z], zs.at[h, j], zr.at[z], CORES * t + core)
+
+    def scatter_chips(h):
+        swap(h).wait_recv()
+        for b, i in enumerate(far_pairs[h]):
+            for t in range(2):
+                j = 2 * b + t
+                sz[h, j] = (xs2[h, core, j].astype(F32) + xr2[h, j].astype(F32)).astype(BF16)
+        for b, i in enumerate(far_pairs[h]):
+            for t in range(2):
+                to = 2 * lax.rem(z // 2 + i, pairs) + t
+                copy = chip_piece(h, 2 * b + t, to)
+                if i:
+                    copy.start()
+                else:
+                    pl.when(to != z)(copy.start)
+
+    def y_piece(t, to):
+        return piece(yg.at[core, t], yg.at[core, t], ys.at[to], yr.at[t], CORES * to + core)
+
+    def gather_early():
+        for i in far[:-1]:
+            t = lax.rem(z + i, chips)
+            piece(rz.at[t], rz.at[t], zs.at[0, 0], zr.at[t], me).wait_recv()
+        total = sz[1, 2 + lax.rem(z, 2)].astype(F32)
+        for i in far[:-1]:
+            total += rz[lax.rem(z + i, chips)].astype(F32)
+        for c in range(early):
+            yg[core, z, c] = (hg[c, me].astype(F32) + total[c]).astype(BF16)
+        for i in far[:-1]:
+            y_piece(z, lax.rem(z + i, chips)).start()
+
+    def forward():
+        return piece(yg.at[core], yg.at[core], fs.at[0], fr.at[0], partner)
+
+    def forward_early():
+        for i in far[:-1]:
+            t = lax.rem(z + i, chips)
+            y_piece(t, t).wait_recv()
+        forward().start()
+
+    def collect_early():
+        forward().wait_recv()
+        for c in range(early):
+            for t in range(chips):
+                both = jnp.concatenate([yg[k, t, c].astype(F32) for k in range(CORES)], 0)
+                out_ref[pl.ds(c * CHUNK, CHUNK), pl.ds(t * cols, cols)] = both.astype(BF16)
 
     def gather2(first, count, send, recv, ssem, rsem, y, gsem, grsem):
         for i in order:
@@ -271,21 +350,35 @@
                 both = jnp.concatenate([y[CORES * t + k, c].astype(F32) for k in range(CORES)], 0)
                 out_ref[pl.ds((first + c) * CHUNK, CHUNK), pl.ds(t * cols, cols)] = both.astype(BF16)
 
-    early = chunks - LATE
-    mlp(0, early, send2, recv2, s2s.at[0], s2r.at[0])
-    mlp(early, LATE, send3, recv3, s2s.at[1], s2r.at[1])
-    gather2(0, early, send2, recv2, s2s.at[0], s2r.at[0], yg, g2s.at[0], g2r.at[0])
-    gather2(early, LATE, send3, recv3, s2s.at[1], s2r.at[1], yh, g2s.at[1], g2r.at[1])
-    collect2(0, early, yg, g2s.at[0], g2r.at[0])
-    collect2(early, LATE, yh, g2s.at[1], g2r.at[1])
+    mlp(0, early, scatter_early)
+    scatter_chips(0)
+    scatter_chips(1)
+    mlp(early, LATE, scatter_late)
+    gather_early()
+    gather2(early, LATE, send3, recv3, s2s, s2r, yh, g2s, g2r)
+    forward_early()
+    collect_early()
+    collect2(early, LATE, yh, g2s, g2r)
 
     for i in order:
         to = peer(i)
         for c in range(chunks):
             piece(hg.at[c, me], hg.at[c, me], g1s.at[c, to], g1r.at[c, me], to).wait_send()
-        for at, send, y in ((0, send2, yg), (1, send3, yh)):
-            piece(send.at[to], send.at[to], s2s.at[at, to], s2r.at[at, me], to).wait_send()
-            piece(y.at[me], y.at[me], g2s.at[at, to], g2r.at[at, me], to).wait_send()
+        piece(send3.at[to], send3.at[to], s2s.at[to], s2r.at[me], to).wait_send()
+        piece(yh.at[me], yh.at[me], g2s.at[to], g2r.at[me], to).wait_send()
+    for h in range(2):
+        swap(h).wait_send()
+        for b, i in enumerate(far_pairs[h]):
+            for t in range(2):
+                to = 2 * lax.rem(z // 2 + i, pairs) + t
+                copy = chip_piece(h, 2 * b + t, to)
+                if i:
+                    copy.wait_send()
+                else:
+                    pl.when(to != z)(copy.wait_send)
+    for i in far[:-1]:
+        y_piece(z, lax.rem(z + i, chips)).wait_send()
+    forward().wait_send()
     for u in range(groups):
         for i in far:
             t = lax.rem(z + i, chips)
@@ -305,6 +398,7 @@
         ff = w_gate.shape[1]
         k_cache, v_cache = k_cache.reshape(rows, cache, HEAD), v_cache.reshape(rows, cache, HEAD)
         chunks, half, cols = rows // CHUNK, CHUNK // CORES, d // (n // CORES)
+        early = (chunks - LATE, half, cols)
         trig = jnp.asarray(rotary_table(cache, HEAD // 2))
         any_, vmem = pl.BlockSpec(memory_space=pl.ANY), pl.BlockSpec(memory_space=pltpu.VMEM)
         dma = pltpu.SemaphoreType.DMA
@@ -330,7 +424,11 @@
                 pltpu.VMEM((rows // GROUP, n // CORES, half, cols), BF16),
                 pltpu.VMEM((chunks, n, half, cols), BF16),
                 pltpu.VMEM((chunks, n, half, cols), BF16),
-                *[pltpu.VMEM((n, chunks - LATE, half, cols), BF16)] * 3,
+                pltpu.VMEM((2, CORES, n // CORES // 2, *early), BF16),
+                pltpu.VMEM((2, n // CORES // 2, *early), BF16),
+                pltpu.VMEM((2, n // CORES // 2, *early), BF16),
+                pltpu.VMEM((n // CORES, *early), BF16),
+                pltpu.VMEM((CORES, n // CORES, *early), BF16),
                 *[pltpu.VMEM((n, LATE, half, cols), BF16)] * 3,
                 dma((6,)),
                 dma((SLOTS,)),
@@ -339,10 +437,11 @@
                 dma((chunks, n)),
                 dma((chunks, n)),
                 dma((chunks, n)),
-                dma((2, n)),
-                dma((2, n)),
-                dma((2, n)),
-                dma((2, n)),
+                *[dma((n,))] * 4,
+                *[dma((2,))] * 2,
+                dma((2, n // CORES // 2)),
+                *[dma((n // CORES,))] * 3,
+                *[dma((1,))] * 2,
             ],
             compiler_params=pltpu.CompilerParams(
                 collective_id=0, has_side_effects=True, vmem_limit_bytes=67_043_328

time: 75.6 us -> 67.6 us (0.89); the launches traced: 74.4 us -> 67.4 us
  Pallas kernels: 72.6 us -> 65.6 us
    pallas_call x1, Pallas kernels: 72.6 us -> 65.6 us  [step(): pl.pallas_call(functools.partial(layer, n), name='layer', out_shape=jax.S...]
where the time goes in v4:
time: 67.6 us; the launch traced here: 67.4 us
  Pallas kernels  65.6 us (97%)
  local copies, waits for them, and re-layouts  1.77 us (3%)
    pallas_call x1, Pallas kernels, step(): pl.pallas_call(functools.partial(layer, n), name='layer', out_shape=jax.S...  65.6 us
    unnamed x1, local copies, waits for them, and re-layouts  1.77 us

profile of v4, /device:TPU:21, one launch (start us, length us, event | category | flops | bytes accessed | tf_op | source)
XLA Modules:
  0.0 67.4 jit_solution(8350301644830275499)
XLA Ops:
  0.0 65.6 %layer.1 = bf16[64,3072]{1,0:T(8,128)(2,1)} custom-call(bf16[64,3072]{1,0:T(8,128)(2,1)} %x_hbm.1, bf16[64,1024,256]{2,1,0:T(8,128)(2,1)} %bitcast.4, bf16[64,1024,256]{2,1,0:T(8,128)(2,1)} %bitcast.5, bf16[24,128]{1,0:T(8,128)(2,1)} %bitcast.6, f32[2,128]{1,0:T(2,128)} %constant.2.clone.trig_ref, bf16[3072,256]{1,0:T(8,128)(2,1)} %wq_hbm.1, ...), custom_call_target="tpu_custom_call" | custom-call | tf_op jit(solution)/shard_map/layer/pallas_call | solution.py:405
  65.7 1.8 %copy.13 = bf16[64,3072]{1,0:T(8,128)(2,1)} copy(bf16[64,3072]{1,0:T(8,128)(2,1)} %layer.1) | data formatting | bytes 786432

commit v5 on v2

v5 whole, which is shorter than its diff:
```python
import functools

import jax
import jax.numpy as jnp
import numpy as np
from jax import lax
from jax.experimental import pallas as pl
from jax.experimental.pallas import tpu as pltpu
from jax.sharding import PartitionSpec as P

HEAD = 256
THETA = 10000
CORES = 2
GROUP = 8
CHUNK = 16
SLOTS = 3
STAGES = 2
MESH = pl.DeviceIdType.MESH
F32, BF16 = jnp.float32, jnp.bfloat16


def rotary_table(cache, half):
    angle = np.float32(cache - 1) * (np.float32(THETA) ** (-np.arange(half, dtype=np.float32) / half))
    return np.stack([np.cos(angle), np.sin(angle)]).astype(np.float32)


def layer(n, x_hbm, k_hbm, v_hbm, ga_ref, trig_ref, wq_hbm, wo_hbm, gm_ref, wg_hbm, wu_hbm, wd_hbm, out_ref,
          x16, xs, a16, wq, wo, wg, wu, wd, kbuf, vbuf, q32, hb,
          send1, recv1, hg, xs2, xr2, sz, rz, yg,
          in_sem, k_sem, v_sem, s1s, s1r, g1s, g1r, xss, xsr, zs, zr, ys, yr, fs, fr):
    rows, d = x16.shape
    ff = wg.shape[1]
    groups, chunks = rows // GROUP, rows // CHUNK
    half = CHUNK // CORES
    chips = n // CORES
    cols = d // chips
    me = lax.axis_index("tp")
    z, core = me // CORES, lax.rem(me, CORES)
    tiles = d // 128

    def peer(i):
        return lax.rem(me + i, n)

    order = sorted(range(1, n), key=lambda i: -min(i, n - i))
    far = [chips // 2]
    for i in range(chips // 2 - 1, 0, -1):
        far += [i, chips - i]
    far.append(0)

    load_x = pltpu.make_async_copy(x_hbm, x16, in_sem.at[0])
    load_wq = pltpu.make_async_copy(wq_hbm, wq, in_sem.at[1])
    load_wo = pltpu.make_async_copy(wo_hbm, wo, in_sem.at[2])
    load_wg = pltpu.make_async_copy(wg_hbm, wg, in_sem.at[3])
    load_wu = pltpu.make_async_copy(wu_hbm, wu, in_sem.at[4])
    load_wd = pltpu.make_async_copy(wd_hbm, wd, in_sem.at[5])

    def load_k(g):
        slot = lax.rem(g, SLOTS)
        return pltpu.make_async_copy(k_hbm.at[pl.ds(g * GROUP, GROUP)], kbuf.at[slot], k_sem.at[slot])

    def load_v(g):
        slot = lax.rem(g, SLOTS)
        return pltpu.make_async_copy(v_hbm.at[pl.ds(g * GROUP, GROUP)], vbuf.at[slot], v_sem.at[slot])

    load_x.start()
    load_wq.start()
    for g in range(SLOTS):
        load_k(g).start()
        load_v(g).start()
        if g == 0:
            load_wo.start()

    barrier = pltpu.get_barrier_semaphore()
    for i in range(1, n):
        pl.semaphore_signal(barrier, inc=1, device_id={"tp": peer(i)}, device_id_type=MESH)

    load_x.wait()
    part = jnp.zeros((rows, 128), F32)
    for j in range(tiles):
        block = x16[:, pl.ds(128 * j, 128)].astype(F32)
        xs[:, pl.ds(128 * j, 128)] = block
        part += block * block
    scale = lax.rsqrt(jnp.sum(part, -1, keepdims=True) / d + 1e-6)
    gain = ga_ref[...].astype(F32)
    for j in range(tiles):
        a16[:, pl.ds(128 * j, 128)] = (xs[:, pl.ds(128 * j, 128)] * scale * gain[j:j + 1]).astype(BF16)
    load_wq.wait()
    q = jnp.dot(a16[...], wq[...], preferred_element_type=F32).astype(BF16).astype(F32)
    turn = HEAD // 2
    cos, sin = trig_ref[0:1], trig_ref[1:2]
    qa, qb = q[:, :turn], q[:, turn:]
    q32[:, :turn] = (qa * cos - qb * sin).astype(BF16).astype(F32)
    q32[:, turn:] = (qb * cos + qa * sin).astype(BF16).astype(F32)

    pl.semaphore_wait(barrier, n - 1)

    def piece(src, dst, ssem, rsem, to):
        return pltpu.make_async_remote_copy(src_ref=src, dst_ref=dst, send_sem=ssem, recv_sem=rsem,
                                            device_id={"tp": to}, device_id_type=MESH)

    def term1(u, seen):
        term = jnp.concatenate([jnp.dot(seen, wo[:, pl.ds(o, 256)], preferred_element_type=F32) for o in range(0, d, 256)], 1)
        for t in range(chips):
            send1[u, t] = term[:, t * cols:(t + 1) * cols].astype(BF16)

    def scatter1(u):
        kind = lax.rem(u, CORES)
        c = u // CORES
        for i in far:
            t = lax.rem(z + i, chips)
            to = CORES * t + kind
            copy = piece(send1.at[u, t], recv1.at[c, me], s1s.at[u, t], s1r.at[c, me], to)
            if i:
                copy.start()
            else:
                pl.when(core != kind)(copy.start)

    def gather1(c):
        u = CORES * c + core
        total = send1[u, z].astype(F32)
        for i in order:
            frm = peer(i)
            piece(send1.at[u, z], recv1.at[c, frm], s1s.at[u, z], s1r.at[c, frm], frm).wait_recv()
        for i in order:
            total += recv1[c, peer(i)].astype(F32)
        at = pl.ds(pl.multiple_of(u * half, half), half)
        hg[c, me] = (xs[at, pl.ds(pl.multiple_of(z * cols, 128), cols)] + total).astype(BF16)
        for i in order:
            to = peer(i)
            piece(hg.at[c, me], hg.at[c, me], g1s.at[c, to], g1r.at[c, me], to).start()

    line = lax.broadcasted_iota(jnp.int32, (GROUP, 1), 0)

    def scores_of(g):
        slot = lax.rem(g, SLOTS)
        qg = q32[pl.ds(pl.multiple_of(g * GROUP, GROUP), GROUP), :]
        lhs = [jnp.where(line == i, qg, 0.0).astype(BF16) for i in range(GROUP)]
        out = []
        for j in range(kbuf.shape[2] // 256):
            total = None
            for i in range(GROUP):
                s = lax.dot_general(lhs[i], kbuf[slot, i, pl.ds(256 * j, 256)], (((1,), (1,)), ((), ())), preferred_element_type=F32)
                total = s if total is None else total + s
            out.append(total)
        return jnp.concatenate(out, 1) * HEAD**-0.5

    def seen_of(g, scores):
        slot = lax.rem(g, SLOTS)
        e = jnp.exp(scores - jnp.max(scores, -1, keepdims=True))
        w = e * (1.0 / jnp.sum(e, -1, keepdims=True))
        lhs = [jnp.where(line == i, w, 0.0).astype(BF16) for i in range(GROUP)]
        out = []
        for j in range(HEAD // 128):
            total = None
            for i in range(GROUP):
                s = jnp.dot(lhs[i], vbuf[slot, i, :, pl.ds(128 * j, 128)], preferred_element_type=F32)
                total = s if total is None else total + s
            out.append(total)
        return jnp.concatenate(out, 1).astype(BF16)

    def attend(g, scores):
        load_v(g).wait()
        load_k(g + 1).wait()
        later = scores_of(g + 1)
        seen = seen_of(g, scores)
        term1(g, seen)

        @pl.when(g + SLOTS < groups)
        def _():
            load_v(g + SLOTS).start()

        @pl.when(g + 1 + SLOTS < groups)
        def _():
            load_k(g + 1 + SLOTS).start()

        @pl.when(g == groups - SLOTS - 1)
        def _():
            load_wg.start()
            load_wu.start()
            load_wd.start()

        scatter1(g)

        @pl.when((lax.rem(g, CORES) == 0) & (g >= 2 * CORES))
        def _():
            gather1(g // CORES - 2)

        return later

    load_k(0).wait()
    scores = scores_of(0)
    load_k(SLOTS).start()
    load_wo.wait()
    scores = lax.fori_loop(0, groups - 1, attend, scores)
    load_v(groups - 1).wait()
    term1(groups - 1, seen_of(groups - 1, scores))
    scatter1(groups - 1)
    for c in range(chunks - 2, chunks):
        gather1(c)

    gain_m = gm_ref[...].astype(F32)
    width = 256

    partner = CORES * z + 1 - core
    others = far[:-1]
    deep = chunks // STAGES

    for c in range(chunks):
        for i in order:
            frm = peer(i)
            piece(hg.at[c, frm], hg.at[c, frm], g1s.at[c, frm], g1r.at[c, frm], frm).wait_recv()
        blocks = []
        part = jnp.zeros((CHUNK, 128), F32)
        for t in range(chips):
            block = jnp.concatenate([hg[c, CORES * t + k].astype(F32) for k in range(CORES)], 0)
            for u in range(cols // 128):
                sub = block[:, 128 * u:128 * (u + 1)]
                blocks.append(sub)
                part += sub * sub
        scale = lax.rsqrt(jnp.sum(part, -1, keepdims=True) / d + 1e-6)
        for j in range(tiles):
            a16[pl.ds(c * CHUNK, CHUNK), pl.ds(128 * j, 128)] = (blocks[j] * scale * gain_m[j:j + 1]).astype(BF16)

    load_wg.wait()
    load_wu.wait()
    for j in range(ff // width):
        at = pl.ds(j * width, width)
        b = a16[...]
        gate = jnp.dot(b, wg[:, at], preferred_element_type=F32)
        up = jnp.dot(b, wu[:, at], preferred_element_type=F32)
        hb[:, at] = (gate / (1.0 + jnp.exp(-gate)) * up).astype(BF16)
    load_wd.wait()

    def swap(s):
        return piece(xs2.at[s, 1 - core], xr2.at[s], xss.at[s], xsr.at[s], partner)

    def chip_piece(s, t):
        return piece(sz.at[s, t], rz.at[s, z], zs.at[s, t], zr.at[s, z], CORES * t + core)

    def y_piece(s, t, to):
        return piece(yg.at[s, core, t], yg.at[s, core, t], ys.at[s, to], yr.at[s, t], CORES * to + core)

    def forward(s):
        return piece(yg.at[s, core], yg.at[s, core], fs.at[s], fr.at[s], partner)

    b = hb[...]
    term = jnp.concatenate([jnp.dot(b, wd[:, pl.ds(o, width)], preferred_element_type=F32).astype(BF16)
                            for o in range(0, d, width)], 1)
    for s in range(STAGES):
        for k in range(CORES):
            for t in range(chips):
                for c in range(deep):
                    row = (s * deep + c) * CHUNK + half * k
                    xs2[s, k, t, c] = term[row:row + half, t * cols:(t + 1) * cols]
        swap(s).start()
    for s in range(STAGES):
        swap(s).wait_recv()
        for t in range(chips):
            sz[s, t] = (xs2[s, core, t].astype(F32) + xr2[s, t].astype(F32)).astype(BF16)
        for i in others:
            chip_piece(s, lax.rem(z + i, chips)).start()
    for s in range(STAGES):
        for i in others:
            t = lax.rem(z + i, chips)
            piece(rz.at[s, t], rz.at[s, t], zs.at[s, t], zr.at[s, t], me).wait_recv()
        total = sz[s, z].astype(F32)
        for i in others:
            total += rz[s, lax.rem(z + i, chips)].astype(F32)
        for c in range(deep):
            yg[s, core, z, c] = (hg[s * deep + c, me].astype(F32) + total[c]).astype(BF16)
        for i in others:
            y_piece(s, z, lax.rem(z + i, chips)).start()
    for s in range(STAGES):
        for i in others:
            t = lax.rem(z + i, chips)
            y_piece(s, t, t).wait_recv()
        forward(s).start()
    for s in range(STAGES):
        forward(s).wait_recv()
        for c in range(deep):
            for t in range(chips):
                both = jnp.concatenate([yg[s, k, t, c].astype(F32) for k in range(CORES)], 0)
                out_ref[pl.ds((s * deep + c) * CHUNK, CHUNK), pl.ds(t * cols, cols)] = both.astype(BF16)

    for i in order:
        to = peer(i)
        for c in range(chunks):
            piece(hg.at[c, me], hg.at[c, me], g1s.at[c, to], g1r.at[c, me], to).wait_send()
    for s in range(STAGES):
        swap(s).wait_send()
        forward(s).wait_send()
        for i in others:
            t = lax.rem(z + i, chips)
            chip_piece(s, t).wait_send()
            y_piece(s, z, t).wait_send()
    for u in range(groups):
        for i in far:
            t = lax.rem(z + i, chips)
            copy = piece(send1.at[u, t], send1.at[u, t], s1s.at[u, t], s1r.at[u // CORES, me], me)
            if i:
                copy.wait_send()
            else:
                pl.when(core != u % CORES)(copy.wait_send)


def solution(mesh):
    n = mesh.shape["tp"]

    def step(x, k_cache, v_cache, gain_a, wq, wo, gain_m, w_gate, w_up, w_down):
        rows, d = x.shape
        cache = k_cache.shape[1]
        ff = w_gate.shape[1]
        k_cache, v_cache = k_cache.reshape(rows, cache, HEAD), v_cache.reshape(rows, cache, HEAD)
        chunks, half, cols = rows // CHUNK, CHUNK // CORES, d // (n // CORES)
        deep = (chunks // STAGES, half, cols)
        trig = jnp.asarray(rotary_table(cache, HEAD // 2))
        any_, vmem = pl.BlockSpec(memory_space=pl.ANY), pl.BlockSpec(memory_space=pltpu.VMEM)
        dma = pltpu.SemaphoreType.DMA
        return pl.pallas_call(
            functools.partial(layer, n),
            name="layer",
            out_shape=pltpu.VMEM((rows, d), BF16),
            in_specs=[any_, any_, any_, vmem, vmem, any_, any_, vmem, any_, any_, any_],
            out_specs=vmem,
            scratch_shapes=[
                pltpu.VMEM((rows, d), BF16),
                pltpu.VMEM((rows, d), F32),
                pltpu.VMEM((rows, d), BF16),
                pltpu.VMEM(wq.shape, BF16),
                pltpu.VMEM(wo.shape, BF16),
                pltpu.VMEM(w_gate.shape, BF16),
                pltpu.VMEM(w_up.shape, BF16),
                pltpu.VMEM(w_down.shape, BF16),
                pltpu.VMEM((SLOTS, GROUP, cache, HEAD), BF16),
                pltpu.VMEM((SLOTS, GROUP, cache, HEAD), BF16),
                pltpu.VMEM((rows, HEAD), F32),
                pltpu.VMEM((rows, ff), BF16),
                pltpu.VMEM((rows // GROUP, n // CORES, half, cols), BF16),
                pltpu.VMEM((chunks, n, half, cols), BF16),
                pltpu.VMEM((chunks, n, half, cols), BF16),
                pltpu.VMEM((STAGES, CORES, n // CORES, *deep), BF16),
                *[pltpu.VMEM((STAGES, n // CORES, *deep), BF16)] * 3,
                pltpu.VMEM((STAGES, CORES, n // CORES, *deep), BF16),
                dma((6,)),
                dma((SLOTS,)),
                dma((SLOTS,)),
                dma((rows // GROUP, n // CORES)),
                dma((chunks, n)),
                dma((chunks, n)),
                dma((chunks, n)),
                *[dma((STAGES,))] * 2,
                *[dma((STAGES, n // CORES))] * 4,
                *[dma((STAGES,))] * 2,
            ],
            compiler_params=pltpu.CompilerParams(
                collective_id=0, has_side_effects=True, vmem_limit_bytes=60 * 1024 * 1024
            ),
        )(x, k_cache, v_cache, gain_a.reshape(-1, 128), trig, wq, wo, gain_m.reshape(-1, 128), w_gate, w_up, w_down)

    states, cache, columns, rows_of = P("dp", None), P("dp", None, "tp", None), P(None, "tp"), P("tp", None)
    return jax.shard_map(
        step,
        mesh=mesh,
        in_specs=(states, cache, cache, P(None), columns, rows_of, P(None), columns, columns, rows_of),
        out_specs=states,
        check_vma=False,
    )
```

time: 80.5 us -> 68.2 us (0.85)
  Pallas kernels: 78.4 us -> 67.3 us
  local copies, waits for them, and re-layouts: 1.77 us -> 0.75 us
    pallas_call x1, Pallas kernels: 78.4 us -> 67.3 us  [step(): pl.pallas_call(functools.partial(layer, n), name='layer', out_shape=pltpu...]
    unnamed x1, local copies, waits for them, and re-layouts: 1.77 us -> 0.75 us
where the time goes in v5:
time: 68.2 us; the launch traced here: 68.1 us
  Pallas kernels  67.3 us (99%)
  local copies, waits for them, and re-layouts  0.75 us (1%)
    pallas_call x1, Pallas kernels, step(): pl.pallas_call(functools.partial(layer, n), name='layer', out_shape=pltpu...  67.3 us

profile of v5, /device:TPU:21, one launch (start us, length us, event | category | flops | bytes accessed | tf_op | source)
XLA Modules:
  0.0 68.1 jit_solution(14655447668644721240)
XLA Ops:
  0.0 67.3 %layer.1 = bf16[64,3072]{1,0:T(8,128)(2,1)S(1)} custom-call(bf16[64,3072]{1,0:T(8,128)(2,1)} %x_hbm.1, bf16[64,1024,256]{2,1,0:T(8,128)(2,1)} %bitcast.4, bf16[64,1024,256]{2,1,0:T(8,128)(2,1)} %bitcast.5, bf16[24,128]{1,0:T(8,128)(2,1)} %bitcast.6, f32[2,128]{1,0:T(2,128)} %constant.2.clone.trig_ref, bf16[3072,256]{1,0:T(8,128)(2,1)} %wq_hbm.1, ...), custom_call_target="tpu_custom_call" | custom-call | tf_op jit(solution)/shard_map/layer/pallas_call | solution.py:319
  67.3 0.7 %copy.13 = bf16[64,3072]{1,0:T(8,128)(2,1)} copy(bf16[64,3072]{1,0:T(8,128)(2,1)S(1)} %layer.1) | data formatting | bytes 786432

commit v6 on v4

--- a/solution.py
+++ b/solution.py
@@ -86,14 +86,13 @@
     for j in range(tiles):
         a16[:, pl.ds(128 * j, 128)] = (xs[:, pl.ds(128 * j, 128)] * scale * gain[j:j + 1]).astype(BF16)
     load_wq.wait()
-    q = jnp.dot(a16[...], wq[...], preferred_element_type=F32).astype(BF16).astype(F32)
+    q = [jnp.dot(a16[...], wq[:, pl.ds(o, 128)], preferred_element_type=F32).astype(BF16).astype(F32) for o in range(0, HEAD, 128)]
+    q = jnp.concatenate(q, 1)
     turn = HEAD // 2
     cos, sin = trig_ref[0:1], trig_ref[1:2]
     qa, qb = q[:, :turn], q[:, turn:]
     q32[:, :turn] = (qa * cos - qb * sin).astype(BF16).astype(F32)
     q32[:, turn:] = (qb * cos + qa * sin).astype(BF16).astype(F32)
-
-    pl.semaphore_wait(barrier, n - 1)
 
     def piece(src, dst, ssem, rsem, to):
         return pltpu.make_async_remote_copy(src_ref=src, dst_ref=dst, send_sem=ssem, recv_sem=rsem,
@@ -177,8 +176,6 @@
         @pl.when(g == groups - SLOTS - 1)
         def _():
             load_wg.start()
-            load_wu.start()
-            load_wd.start()
 
         scatter1(g)
 
@@ -192,12 +189,15 @@
     scores = scores_of(0)
     load_k(SLOTS).start()
     load_wo.wait()
+    pl.semaphore_wait(barrier, n - 1)
     scores = lax.fori_loop(0, groups - 1, attend, scores)
     load_v(groups - 1).wait()
     term1(groups - 1, seen_of(groups - 1, scores))
     scatter1(groups - 1)
-    for c in range(chunks - 2, chunks):
-        gather1(c)
+    gather1(chunks - 2)
+    load_wu.start()
+    gather1(chunks - 1)
+    load_wd.start()
 
     gain_m = gm_ref[...].astype(F32)
     width = 256
@@ -405,7 +405,7 @@
         return pl.pallas_call(
             functools.partial(layer, n),
             name="layer",
-            out_shape=jax.ShapeDtypeStruct((rows, d), BF16),
+            out_shape=pltpu.VMEM((rows, d), BF16),
             in_specs=[any_, any_, any_, vmem, vmem, any_, any_, vmem, any_, any_, any_],
             out_specs=vmem,
             scratch_shapes=[
@@ -444,7 +444,7 @@
                 *[dma((1,))] * 2,
             ],
             compiler_params=pltpu.CompilerParams(
-                collective_id=0, has_side_effects=True, vmem_limit_bytes=67_043_328
+                collective_id=0, has_side_effects=True, vmem_limit_bytes=60 * 1024 * 1024
             ),
         )(x, k_cache, v_cache, gain_a.reshape(-1, 128), trig, wq, wo, gain_m.reshape(-1, 128), w_gate, w_up, w_down)
 

time: 67.6 us -> 65.1 us (0.963)
  the two profiles are of different devices: /device:TPU:21 before, /device:TPU:31 now
where the time goes in v6:
time: 65.1 us; the launch traced here: 65 us
  Pallas kernels  64.2 us (99%)
  local copies, waits for them, and re-layouts  0.75 us (1%)
    pallas_call x1, Pallas kernels, step(): pl.pallas_call(functools.partial(layer, n), name='layer', out_shape=pltpu...  64.2 us

profile of v6, /device:TPU:31, one launch (start us, length us, event | category | flops | bytes accessed | tf_op | source)
XLA Modules:
  0.0 65.0 jit_solution(14260499253253550968)
XLA Ops:
  0.0 64.2 %layer.1 = bf16[64,3072]{1,0:T(8,128)(2,1)S(1)} custom-call(bf16[64,3072]{1,0:T(8,128)(2,1)} %x_hbm.1, bf16[64,1024,256]{2,1,0:T(8,128)(2,1)} %bitcast.4, bf16[64,1024,256]{2,1,0:T(8,128)(2,1)} %bitcast.5, bf16[24,128]{1,0:T(8,128)(2,1)} %bitcast.6, f32[2,128]{1,0:T(2,128)} %constant.2.clone.trig_ref, bf16[3072,256]{1,0:T(8,128)(2,1)} %wq_hbm.1, ...), custom_call_target="tpu_custom_call" | custom-call | tf_op jit(solution)/shard_map/layer/pallas_call | solution.py:405
  64.2 0.7 %copy.13 = bf16[64,3072]{1,0:T(8,128)(2,1)} copy(bf16[64,3072]{1,0:T(8,128)(2,1)S(1)} %layer.1) | data formatting | bytes 786432

commit v7 on v6

--- a/solution.py
+++ b/solution.py
@@ -52,7 +52,10 @@
     load_wq = pltpu.make_async_copy(wq_hbm, wq, in_sem.at[1])
     load_wo = pltpu.make_async_copy(wo_hbm, wo, in_sem.at[2])
     load_wg = pltpu.make_async_copy(wg_hbm, wg, in_sem.at[3])
-    load_wu = pltpu.make_async_copy(wu_hbm, wu, in_sem.at[4])
+    top = pl.ds(0, d // 2)
+    bottom = pl.ds(d // 2, d // 2)
+    load_wu = pltpu.make_async_copy(wu_hbm.at[top], wu.at[top], in_sem.at[4])
+    load_wu2 = pltpu.make_async_copy(wu_hbm.at[bottom], wu.at[bottom], in_sem.at[6])
     load_wd = pltpu.make_async_copy(wd_hbm, wd, in_sem.at[5])
 
     def load_k(g):
@@ -165,6 +168,8 @@
         seen = seen_of(g, scores)
         term1(g, seen)
 
+        scatter1(g)
+
         @pl.when(g + SLOTS < groups)
         def _():
             load_v(g + SLOTS).start()
@@ -176,8 +181,7 @@
         @pl.when(g == groups - SLOTS - 1)
         def _():
             load_wg.start()
-
-        scatter1(g)
+            load_wu.start()
 
         @pl.when((lax.rem(g, CORES) == 0) & (g >= 2 * CORES))
         def _():
@@ -195,7 +199,7 @@
     term1(groups - 1, seen_of(groups - 1, scores))
     scatter1(groups - 1)
     gather1(chunks - 2)
-    load_wu.start()
+    load_wu2.start()
     gather1(chunks - 1)
     load_wd.start()
 
@@ -229,6 +233,7 @@
         if first == 0:
             load_wg.wait()
             load_wu.wait()
+            load_wu2.wait()
 
         def hidden(j, _):
             at = pl.ds(pl.multiple_of(j * width, width), width)
@@ -430,7 +435,7 @@
                 pltpu.VMEM((n // CORES, *early), BF16),
                 pltpu.VMEM((CORES, n // CORES, *early), BF16),
                 *[pltpu.VMEM((n, LATE, half, cols), BF16)] * 3,
-                dma((6,)),
+                dma((7,)),
                 dma((SLOTS,)),
                 dma((SLOTS,)),
                 dma((rows // GROUP, n // CORES)),

time: 65.1 us -> 65.2 us (level)
  the two profiles are of different devices: /device:TPU:31 before, /device:TPU:21 now
where the time goes in v7:
time: 65.2 us; the launch traced here: 65.1 us
  Pallas kernels  64.3 us (99%)
  local copies, waits for them, and re-layouts  0.75 us (1%)
    pallas_call x1, Pallas kernels, step(): pl.pallas_call(functools.partial(layer, n), name='layer', out_shape=pltpu...  64.3 us

profile of v7, /device:TPU:21, one launch (start us, length us, event | category | flops | bytes accessed | tf_op | source)
XLA Modules:
  0.0 65.1 jit_solution(11670713524380401305)
XLA Ops:
  0.0 64.3 %layer.1 = bf16[64,3072]{1,0:T(8,128)(2,1)S(1)} custom-call(bf16[64,3072]{1,0:T(8,128)(2,1)} %x_hbm.1, bf16[64,1024,256]{2,1,0:T(8,128)(2,1)} %bitcast.4, bf16[64,1024,256]{2,1,0:T(8,128)(2,1)} %bitcast.5, bf16[24,128]{1,0:T(8,128)(2,1)} %bitcast.6, f32[2,128]{1,0:T(2,128)} %constant.2.clone.trig_ref, bf16[3072,256]{1,0:T(8,128)(2,1)} %wq_hbm.1, ...), custom_call_target="tpu_custom_call" | custom-call | tf_op jit(solution)/shard_map/layer/pallas_call | solution.py:410
  64.3 0.7 %copy.13 = bf16[64,3072]{1,0:T(8,128)(2,1)} copy(bf16[64,3072]{1,0:T(8,128)(2,1)S(1)} %layer.1) | data formatting | bytes 786432
